TPU v7x, 32 devices: a whole 2x2x4 slice. The times are simulated.
32 devices in a mesh: node: 16 (over z, y, core), ell: 2 (over x).
Axes of the slice: x: 2, y: 2, z: 4, core: 2. Of those that a mesh axis runs over, the one named last changes fastest.
Arguments:
- table_zero: bfloat16 [6144, 1536], P('node', 'ell'), may hold values from -1 to 1
- table_two: bfloat16 [6144, 1536], P('node', 'ell'), may hold values from -1 to 1
- spectrum: bfloat16 [1536], P('ell'), may hold values from -0.15625 to 0.15625
- weights: float32 [6144], P('node'), may hold values from 0.02551552 to 0.25515518
Outputs:
- kernel: float32 [1536, 1536], P('node', 'ell')
All inputs are finite; a program needn't handle non-finite values.
Results may differ from a plain program's by a relative error of at most 0.0029.
Values may be sent and summed in bfloat16 or wider, within the bound.
A program may use at most 128 MiB of HBM per device.

v0:
```python
import jax
import jax.numpy as jnp
from jax import lax
from jax.sharding import PartitionSpec as P


def contract_nodes(left, right):
    return lax.dot_general(
        left, right, (((0,), (0,)), ((), ())), preferred_element_type=jnp.float32
    )


def per_device(table_zero, table_two, spectrum, weights):
    partial_value = jnp.dot(table_zero, spectrum, preferred_element_type=jnp.float32)
    xi = lax.psum(partial_value, "ell")
    gathered = lax.all_gather(table_zero, "ell", axis=1, tiled=True)
    weighted = ((weights * xi)[:, None] * gathered.astype(jnp.float32)).astype(jnp.bfloat16)
    return lax.psum_scatter(
        contract_nodes(weighted, table_two), "node", scatter_dimension=0, tiled=True
    )


def solution(mesh):
    placed = (P("node", "ell"), P("node", "ell"), P("ell"), P("node"))
    return jax.shard_map(
        per_device, mesh=mesh, in_specs=placed, out_specs=P("node", "ell"), check_vma=False
    )
```

profile of v0, /device:TPU:0, one launch (start us, length us, event | category | flops | bytes accessed | tf_op | source)
XLA Modules:
  0.0 121.9 jit_solution(10760141810804105223)
XLA Ops:
  6.5 0.0 copy-start
  6.5 0.0 all-gather.2.cloned.1.call-start
  6.5 0.7 all-gather.2.cloned.1.call-update
  7.3 0.0 reduce-scatter.2.cloned.1.call-start
  7.3 0.7 reshape.1
  8.0 1.4 %convolution_reduce_fusion = f32[384]{0:T(512)S(1)} fusion(bf16[384,768]{1,0:T(8,128)(2,1)} %param.4, bf16[768,1]{0,1:T(2,128)(2,1)S(1)} %reshape.1), kind=kOutput, calls=%fused_computation.3 | convolution fusion | flops 589824 | bytes 592896 | tf_op jit(solution)/shard_map/dot_general | solution.py:14
  9.3 5.8 %psum.7 = f32[384]{0:T(512)S(1)} all-reduce(f32[384]{0:T(512)S(1)} %convolution_reduce_fusion), channel_id=1, replica_groups=mesh['node'=16,'ell'=2] {'ell'}, use_global_device_ids=true, to_apply=%region_0.0 | all-reduce | flops 384 | bytes 3072 | tf_op jit(solution)/shard_map/psum | solution.py:15
  15.2 0.7 mul.11
  15.9 18.5 %all-gather.2.cloned.1.call-done = bf16[384,1536]{1,0:T(8,128)(2,1)} async-done(((bf16[384,768]{1,0:T(8,128)(2,1)}), bf16[384,1536]{1,0:T(8,128)(2,1)}) %all-gather.2.cloned.1.call-update) | async-done | bytes 1179664 | tf_op jit(solution)/shard_map/all_gather | solution.py:16
  34.4 0.0 copy-done
  34.4 4.9 %fusion = f32[1536,768]{1,0:T(8,128)} fusion(bf16[384,768]{1,0:T(8,128)(2,1)S(1)} %copy-done, bf16[384,1536]{1,0:T(8,128)(2,1)} %all-gather.2.cloned.1.call-done, f32[384]{0:T(512)S(1)} %mul.11), kind=kOutput, calls=%fused_computation.1 | convolution fusion | flops 907739136 | bytes 6489600 | tf_op jit(solution)/shard_map/dot_general | solution.py:8
  39.3 0.0 reduce-scatter.2.cloned.1.call-update
  39.3 75.7 %reduce-scatter.2.cloned.1.call-done = f32[96,768]{1,0:T(8,128)} async-done(((f32[1536,768]{1,0:T(8,128)}), f32[96,768]{1,0:T(8,128)}) %reduce-scatter.2.cloned.1.call-update) | async-done | bytes 294928 | tf_op jit(solution)/shard_map/reduce_scatter | solution.py:18
Async XLA Ops:
  6.5 27.9 %copy-start = (bf16[384,768]{1,0:T(8,128)(2,1)S(1)}, bf16[384,768]{1,0:T(8,128)(2,1)}, u32[]{:S(2)}) copy-start(bf16[384,768]{1,0:T(8,128)(2,1)} %param.5) | copy-start | bytes 1769476
  6.5 27.8 %all-gather.2.cloned.1.call-start = ((), (), s32[]{:S(2)}) async-start(), calls=%async_computation.1 | async-start | bytes 1769472 | tf_op jit(solution)/shard_map/all_gather | solution.py:16
  7.3 107.8 %reduce-scatter.2.cloned.1.call-start = ((), (), s32[]{:S(2)}) async-start(), calls=%async_computation.2 | async-start | bytes 5013504 | tf_op jit(solution)/shard_map/reduce_scatter | solution.py:18
Sparse Core Ops, SparseCore 0:
  8.9 25.4 all-gather.1
  39.4 75.5 reduce-scatter.1
where the time goes:
time: 122 us
  waiting for transfers between devices  94.9 us (78%)
  between operations  13.4 us (11%)
  matrix products  6.26 us (5%)
  blocking collectives  5.85 us (5%)
    reduce_scatter x1, waiting for transfers between devices, per_device(): lax.psum_scatter(contract_nodes(weighted, table_two), 'node', scatter_dim...  75.7 us
    all_gather x1, waiting for transfers between devices, per_device(): gathered = lax.all_gather(table_zero, 'ell', axis=1, tiled=True)  18.5 us
    psum x1, blocking collectives, per_device(): xi = lax.psum(partial_value, 'ell')  5.85 us
    dot_general x1, matrix products, contract_nodes(): lax.dot_general(left, right, (((0,), (0,)), ((), ())), preferred_element_...  4.9 us
  transfers between devices with their start and end apart: 2, of which 2 were waited for; matrix products, arithmetic and copies ran while one was open for 2% of the time, Pallas kernels for 0%

commit v1 on v0

--- a/solution.py
+++ b/solution.py
@@ -13,7 +13,7 @@
 def per_device(table_zero, table_two, spectrum, weights):
     partial_value = jnp.dot(table_zero, spectrum, preferred_element_type=jnp.float32)
     xi = lax.psum(partial_value, "ell")
-    gathered = lax.all_gather(table_zero, "ell", axis=1, tiled=True)
+    gathered = jnp.concatenate(lax.all_gather(table_zero, "ell"), axis=1)
     weighted = ((weights * xi)[:, None] * gathered.astype(jnp.float32)).astype(jnp.bfloat16)
     return lax.psum_scatter(
         contract_nodes(weighted, table_two), "node", scatter_dimension=0, tiled=True

time: 122 us -> 126 us (1.033)
  other arithmetic: 0.68 us -> 3.73 us
  local copies, waits for them, and re-layouts: 0.69 us -> 2.72 us
  matrix products: 6.26 us -> 4.87 us
    convert_element_type x0 -> x2, other arithmetic: none -> 3.04 us  [the longest x1 2.85 us: per_device(): gathered.astype(jnp.float32)]
    convert_element_type x0 -> x1, local copies, waits for them, and re-layouts: none -> 2.03 us  [per_device(): gathered.astype(jnp.float32)]
    dot_general x1, matrix products: 4.9 us -> 3.52 us  [contract_nodes(): lax.dot_general(left, right, (((0,), (0,)), ((), ())), preferred_element_...]
where the time goes in v1:
time: 126 us
  waiting for transfers between devices  94.9 us (75%)
  between operations  13.4 us (11%)
  blocking collectives  5.85 us (5%)
  matrix products  4.87 us (4%)
  other arithmetic  3.73 us (3%)
  local copies, waits for them, and re-layouts  2.72 us (2%)
    reduce_scatter x1, waiting for transfers between devices, per_device(): lax.psum_scatter(contract_nodes(weighted, table_two), 'node', scatter_dim...  75.7 us
    all_gather x1, waiting for transfers between devices, per_device(): gathered = jnp.concatenate(lax.all_gather(table_zero, 'ell'), axis=1)  18.5 us
    psum x1, blocking collectives, per_device(): xi = lax.psum(partial_value, 'ell')  5.85 us
    dot_general x1, matrix products, contract_nodes(): lax.dot_general(left, right, (((0,), (0,)), ((), ())), preferred_element_...  3.52 us
    convert_element_type x1, other arithmetic, per_device(): gathered.astype(jnp.float32)  2.85 us
  transfers between devices with their start and end apart: 2, of which 2 were waited for; matrix products, arithmetic and copies ran while one was open for 2% of the time, Pallas kernels for 0%

profile of v1, /device:TPU:0, one launch (start us, length us, event | category | flops | bytes accessed | tf_op | source)
XLA Modules:
  0.0 125.6 jit_solution(16815173560662781296)
XLA Ops:
  6.5 0.0 copy-start
  6.5 0.0 all-gather.3.cloned.1.call-start
  6.5 0.7 all-gather.3.cloned.1.call-update
  7.3 0.0 reduce-scatter.2.cloned.1.call-start
  7.3 0.7 reshape.8
  8.0 1.4 %convolution_reduce_fusion = f32[384]{0:T(512)S(1)} fusion(bf16[384,768]{1,0:T(8,128)(2,1)} %param.4, bf16[768,1]{0,1:T(2,128)(2,1)S(1)} %reshape.8), kind=kOutput, calls=%fused_computation.3 | convolution fusion | flops 589824 | bytes 592896 | tf_op jit(solution)/shard_map/dot_general | solution.py:14
  9.3 5.8 %psum.7 = f32[384]{0:T(512)S(1)} all-reduce(f32[384]{0:T(512)S(1)} %convolution_reduce_fusion), channel_id=1, replica_groups=mesh['node'=16,'ell'=2] {'ell'}, use_global_device_ids=true, to_apply=%region_0.0 | all-reduce | flops 384 | bytes 3072 | tf_op jit(solution)/shard_map/psum | solution.py:15
  15.2 0.7 mul.11
  15.9 18.5 %all-gather.3.cloned.1.call-done = bf16[768,768]{1,0:T(8,128)(2,1)} async-done(((bf16[384,768]{1,0:T(8,128)(2,1)}), bf16[768,768]{1,0:T(8,128)(2,1)}) %all-gather.3.cloned.1.call-update) | async-done | bytes 1179664 | tf_op jit(solution)/shard_map/all_gather | solution.py:16
  34.4 2.9 %convert_bitcast_fusion = f32[384,2,768]{2,0,1:T(8,128)} fusion(bf16[2,384,768]{2,1,0:T(8,128)(2,1)} %bitcast.12), kind=kLoop, calls=%fused_computation | loop fusion | flops 589824 | bytes 3538944 | tf_op jit(solution)/shard_map/convert_element_type | solution.py:17
  37.2 2.0 %copy.5 = f32[384,2,768]{0,2,1:T(8,128)S(1)} copy(f32[384,2,768]{2,0,1:T(8,128)} %convert_bitcast_fusion) | data formatting | bytes 4718592 | tf_op jit(solution)/shard_map/convert_element_type | solution.py:17
  39.3 0.2 fusion
  39.5 0.0 copy-done
  39.5 3.5 %fusion.1 = f32[1536,768]{1,0:T(8,128)} fusion(bf16[384,1536]{0,1:T(8,128)(2,1)S(1)} %fusion, bf16[384,768]{1,0:T(8,128)(2,1)S(1)} %copy-done), kind=kOutput, calls=%fused_computation.4 | convolution fusion | flops 905969664 | bytes 6488064 | tf_op jit(solution)/shard_map/dot_general | solution.py:8
  43.0 0.0 reduce-scatter.2.cloned.1.call-update
  43.0 75.7 %reduce-scatter.2.cloned.1.call-done = f32[96,768]{1,0:T(8,128)} async-done(((f32[1536,768]{1,0:T(8,128)}), f32[96,768]{1,0:T(8,128)}) %reduce-scatter.2.cloned.1.call-update) | async-done | bytes 294928 | tf_op jit(solution)/shard_map/reduce_scatter | solution.py:18
Async XLA Ops:
  6.5 32.9 %copy-start = (bf16[384,768]{1,0:T(8,128)(2,1)S(1)}, bf16[384,768]{1,0:T(8,128)(2,1)}, u32[]{:S(2)}) copy-start(bf16[384,768]{1,0:T(8,128)(2,1)} %param.5) | copy-start | bytes 1769476
  6.5 27.8 %all-gather.3.cloned.1.call-start = ((), (), s32[]{:S(2)}) async-start(), calls=%async_computation.2 | async-start | bytes 1769472 | tf_op jit(solution)/shard_map/all_gather | solution.py:16
  7.3 111.5 %reduce-scatter.2.cloned.1.call-start = ((), (), s32[]{:S(2)}) async-start(), calls=%async_computation.1 | async-start | bytes 5013504 | tf_op jit(solution)/shard_map/reduce_scatter | solution.py:18
Sparse Core Ops, SparseCore 0:
  8.9 25.4 all-gather.2
  43.1 75.5 reduce-scatter.1
